TPU v7x, 32 devices: a whole 2x2x4 slice. The times are simulated.
32 devices in a mesh: dp: 1, ep: 32 (over x, y, z, core).
Axes of the slice: x: 2, y: 2, z: 4, core: 2. Of those that a mesh axis runs over, the one named last changes fastest.
Arguments:
- x: bfloat16 [1, 32, 256, 1536], P('dp', 'ep')
- expert: int32 [1, 32, 256, 2], P('dp', 'ep')
- slot: int32 [1, 32, 256, 2], P('dp', 'ep')
- gate: float32 [1, 32, 256, 2], P('dp', 'ep')
- w_gate: bfloat16 [32, 1536, 9216], P('ep')
- w_up: bfloat16 [32, 1536, 9216], P('ep')
- w_down: bfloat16 [32, 9216, 1536], P('ep')
Outputs:
- y: bfloat16 [1, 32, 256, 1536], P('dp', 'ep')
All inputs are finite; a program needn't handle non-finite values.
Results may differ from a plain program's by a relative error of at most 0.009.
Values are sent between devices in bfloat16 or wider.
A program may use at most 2 GiB of HBM per device.

v0:
```python
import jax
import jax.numpy as jnp
from jax import lax
from jax.sharding import NamedSharding, PartitionSpec as P


def einsum(form, a, b):
    return jnp.einsum(form, a.astype(jnp.float32), b.astype(jnp.float32))


def solution(mesh):
    def placed(v, *spec):
        return lax.with_sharding_constraint(v, NamedSharding(mesh, P(*spec)))

    def step(x, expert, slot, gate, w_gate, w_up, w_down):
        experts, (tokens, top) = w_gate.shape[0], expert.shape[2:]
        slots = 5 * tokens * top // (4 * experts)
        to_expert = jax.nn.one_hot(expert, experts, dtype=jnp.bfloat16)
        to_slot = jax.nn.one_hot(slot, slots, dtype=jnp.bfloat16)
        weighted = to_expert * gate[..., None].astype(jnp.bfloat16)
        dispatch = einsum("abtke,abtkc->abtec", to_expert, to_slot).astype(jnp.bfloat16)
        combine = einsum("abtke,abtkc->abtec", weighted, to_slot).astype(jnp.bfloat16)
        z = einsum("abtec,abtd->aebcd", dispatch, x).astype(jnp.bfloat16)
        z = placed(z, "dp", None, "ep", None, None)
        z = placed(z, "dp", "ep", None, None, None)
        h = jax.nn.silu(einsum("aebcd,edf->aebcf", z, w_gate))
        h = (h * einsum("aebcd,edf->aebcf", z, w_up)).astype(jnp.bfloat16)
        out = einsum("aebcf,efd->aebcd", h, w_down).astype(jnp.bfloat16)
        out = placed(out, "dp", "ep", None, None, None)
        out = placed(out, "dp", None, "ep", None, None)
        y = einsum("abtec,aebcd->abtd", combine, out)
        return y.astype(jnp.bfloat16)

    return step
```

profile of v0, /device:TPU:0, one launch (start us, length us, event | category | flops | bytes accessed | tf_op | source)
XLA Modules:
  0.0 217.9 jit_solution(14487006960768655793)
XLA Ops:
  0.0 0.0 copy-start
  0.0 0.9 copy.3
  0.9 0.0 copy-start.2
  0.9 0.8 copy.5
  1.7 0.0 copy-done.2
  1.8 0.0 copy-start.4
  1.8 0.6 copy-done.4
  2.4 2.8 %fusion.40 = bf16[256,32,20]{1,2,0:T(8,128)(2,1)S(1)} fusion(s32[256,2]{1,0:T(8,128)S(1)} %copy.5, s32[256,2]{1,0:T(8,128)S(1)} %copy.3), kind=kOutput, calls=%fused_computation.29 | convolution fusion | flops 681984 | bytes 331776 | tf_op jit(solution)/abtke,abtkc->abtec/dot_general | solution.py:8
  5.2 0.9 copy.11
  6.1 0.0 copy-done
  6.1 0.7 fusion.23
  6.7 1.1 copy.6
  7.8 64.2 %all-to-all.4 = bf16[1,32,1,1,20,1536]{5,4,3,2,0,1:T(8,128)(2,1)S(1)} all-to-all(bf16[1,32,1,1,20,1536]{5,4,3,2,0,1:T(8,128)(2,1)S(1)} %copy.6), channel_id=1, replica_groups=mesh['dp'=1,'ep'=32] {'ep'}, dimensions={1} | all-to-all | bytes 3932160 | tf_op jit(solution)/sharding_constraint;jit(solution)/sharding_constraint | solution.py:13
  72.1 25.8 %fusion.4 = f32[32,20,9216]{2,0,1:T(8,128)} fusion(bf16[1,1536,9216]{2,1,0:T(8,128)(2,1)} %param.4, bf16[1,32,1,1,20,1536]{5,4,3,2,0,1:T(8,128)(2,1)S(1)} %all-to-all.4), kind=kOutput, calls=%fused_computation.4 | convolution fusion | flops 18119393280 | bytes 53870592 | tf_op jit(solution)/aebcd,edf->aebcf/dot_general | solution.py:8
  97.9 34.7 %fusion.12.clone.8 = bf16[32,20,9216]{2,0,1:T(8,128)(2,1)} fusion(bf16[1,1536,9216]{2,1,0:T(8,128)(2,1)} %param.5, f32[32,20,9216]{2,0,1:T(8,128)} %fusion.4, bf16[1,32,1,1,20,1536]{5,4,3,2,0,1:T(8,128)(2,1)S(1)} %all-to-all.4), kind=kOutput, calls=%fused_computation.13.clone.clone.clone.clone.clone.clone.clone.1 | convolution fusion | flops 18154782720 | bytes 65667072 | tf_op jit(solution)/aebcd,edf->aebcf/dot_general | solution.py:8
  132.6 0.0 copy-start.6
  132.6 0.0 copy-start.3
  132.6 0.0 copy-start.5
  132.6 23.3 %fusion.24 = bf16[1,1,32,1,20,1536]{5,2,4,3,1,0:T(8,128)(2,1)S(1)} fusion(bf16[1,9216,1536]{2,1,0:T(8,128)(2,1)} %param.6, bf16[32,20,9216]{2,0,1:T(8,128)(2,1)} %fusion.12.clone.8), kind=kOutput, calls=%fused_computation.18 | convolution fusion | flops 18120376320 | bytes 42074112 | tf_op jit(solution)/aebcf,efd->aebcd/dot_general | solution.py:8
  156.0 2.5 %copy.8 = bf16[1,1,32,1,20,1536]{5,4,3,1,0,2:T(8,128)(2,1)} copy(bf16[1,1,32,1,20,1536]{5,2,4,3,1,0:T(8,128)(2,1)S(1)} %fusion.24) | data formatting | bytes 3932160 | tf_op jit(solution)/sharding_constraint;jit(solution)/sharding_constraint | solution.py:13
  158.5 2.8 %all-to-all-start.1 = ((bf16[1,1,32,1,20,1536]{5,4,3,1,0,2:T(8,128)(2,1)}), bf16[1,1,32,1,20,1536]{5,4,3,1,0,2:T(8,128)(2,1)S(1)}, u32[]{:S(2)}, u32[]{:S(2)}) async-start(bf16[1,1,32,1,20,1536]{5,4,3,1,0,2:T(8,128)(2,1)} %copy.8), calls=%async_computation.1 | async-start | bytes 4718592 | tf_op jit(solution)/sharding_constraint;jit(solution)/sharding_constraint | solution.py:13
  161.2 0.0 copy-done.6
  161.2 0.0 copy-start.1
  161.3 0.1 copy.4
  161.4 0.0 copy-done.3
  161.4 0.0 copy-done.5
  161.4 3.9 %fusion.43 = bf16[256,32,20]{1,2,0:T(8,128)(2,1)} fusion(s32[256,2]{1,0:T(8,128)S(1)} %copy-done.5, s32[256,2]{1,0:T(8,128)S(1)} %copy-done.3, bf16[256,2]{1,0:T(8,128)(2,1)S(1)} %copy.4), kind=kOutput, calls=%fused_computation.32 | convolution fusion | flops 698368 | bytes 332800 | tf_op jit(solution)/abtke,abtkc->abtec/dot_general | solution.py:8
  165.3 1.9 copy.10
  167.2 49.0 %all-to-all-done.1 = bf16[1,1,32,1,20,1536]{5,4,3,1,0,2:T(8,128)(2,1)S(1)} async-done(((bf16[1,1,32,1,20,1536]{5,4,3,1,0,2:T(8,128)(2,1)}), bf16[1,1,32,1,20,1536]{5,4,3,1,0,2:T(8,128)(2,1)S(1)}, u32[]{:S(2)}, u32[]{:S(2)}) %all-to-all-start.1) | async-done | bytes 1966112 | tf_op jit(solution)/sharding_constraint;jit(solution)/sharding_constraint | solution.py:13
  216.2 1.7 fusion.30
  217.9 0.0 copy-done.1
  (1 shorter events, 0.0 us)
Async XLA Ops:
  0.0 6.1 %copy-start = (bf16[1,1,256,1536]{3,2,1,0:T(8,128)(2,1)S(1)}, bf16[1,1,256,1536]{3,2,1,0:T(8,128)(2,1)}, u32[]{:S(2)}) copy-start(bf16[1,1,256,1536]{3,2,1,0:T(8,128)(2,1)} %param.3) | copy-start | bytes 2359300
  0.9 0.9 copy-start.2
  1.8 0.7 copy-start.4
  132.6 28.6 %copy-start.6 = (f32[1,1,256,2]{2,3,1,0:T(2,128)S(1)}, f32[1,1,256,2]{2,3,1,0:T(2,128)}, u32[]{:S(2)}) copy-start(f32[1,1,256,2]{2,3,1,0:T(2,128)} %param.1) | copy-start | bytes 6148
  132.6 28.8 %copy-start.3 = (s32[256,2]{1,0:T(8,128)S(1)}, s32[256,2]{1,0:T(8,128)}, u32[]{:S(2)}) copy-start(s32[256,2]{1,0:T(8,128)} %copy-done.2) | copy-start | bytes 6148
  132.6 28.8 %copy-start.5 = (s32[256,2]{1,0:T(8,128)S(1)}, s32[256,2]{1,0:T(8,128)}, u32[]{:S(2)}) copy-start(s32[256,2]{1,0:T(8,128)} %copy-done.4) | copy-start | bytes 6148
  158.5 57.7 %all-to-all-start.1 = ((bf16[1,1,32,1,20,1536]{5,4,3,1,0,2:T(8,128)(2,1)}), bf16[1,1,32,1,20,1536]{5,4,3,1,0,2:T(8,128)(2,1)S(1)}, u32[]{:S(2)}, u32[]{:S(2)}) async-start(bf16[1,1,32,1,20,1536]{5,4,3,1,0,2:T(8,128)(2,1)} %copy.8), calls=%async_computation.1 | async-start | bytes 4718592 | tf_op jit(solution)/sharding_constraint;jit(solution)/sharding_constraint | solution.py:13
  161.2 56.7 %copy-start.1 = (bf16[1,1,256,1536]{3,2,1,0:T(8,128)(2,1)S(1)}, bf16[1,1,256,1536]{3,2,1,0:T(8,128)(2,1)}, u32[]{:S(2)}) copy-start(bf16[1,1,256,1536]{3,2,1,0:T(8,128)(2,1)} %param.3) | copy-start | bytes 2359300
where the time goes:
time: 218 us
  matrix products  92.9 us (43%)
  blocking collectives  64.2 us (29%)
  waiting for transfers between devices  49 us (22%)
  local copies, waits for them, and re-layouts  8.85 us (4%)
  starting transfers between devices  2.77 us (1%)
    dot_general x7, matrix products, einsum(): return jnp.einsum(form, a.astype(jnp.float32), b.astype(jnp.float32))  92.9 us
    another operation x1, blocking collectives, placed(): return lax.with_sharding_constraint(v, NamedSharding(mesh, P(*spec)))  64.2 us
    another operation x1, waiting for transfers between devices, placed(): return lax.with_sharding_constraint(v, NamedSharding(mesh, P(*spec)))  49 us
  transfers between devices with their start and end apart: 1, of which 1 were waited for; matrix products, arithmetic and copies ran while one was open for 3% of the time, Pallas kernels for 0%

commit v1 on v0

v1 whole, which is shorter than its diff:
```python
import functools

import jax
import jax.numpy as jnp
from jax import lax
from jax.experimental import pallas as pl
from jax.experimental.pallas import tpu as pltpu
from jax.sharding import PartitionSpec as P

MESH = pl.DeviceIdType.MESH
N = 32
T, D, FF = 256, 1536, 9216
C = 20
Q = D // 4
FT = 512
TILES = FF // FT
DEPTH = 4
BLOCK = 256

MASK_BITS = (0, 3, 4, 1, 2)
NEAR, FAR1, FAR2 = (0, 16, 0), (16, 8, 320), (24, 8, 480)
GROUPS = (NEAR, FAR1, FAR2)


def dot(a, b, contract=((1,), (0,))):
    return lax.dot_general(a, b, (contract, ((), ())), preferred_element_type=jnp.float32)


def partner(me, p):
    out = 0
    for b, bit in enumerate(MASK_BITS):
        mine = lax.rem(me // (1 << bit), 2)
        other = lax.rem(p // (1 << b), 2)
        out += lax.rem(mine + other, 2) * (1 << bit)
    return out


def rows_of(p):
    return pl.multiple_of(p * 16 + 64 * (p // 16) + 32 * (p // 24), 16)


def iota(shape, dim):
    return lax.broadcasted_iota(jnp.int32, shape, dim)


def kernel(x_hbm, e_hbm, s_hbm, g_hbm, wg_hbm, wu_hbm, wd_hbm, y_ref,
           x_ref, e_ref, s_ref, g_ref, zs, zse, z, zre, o, oe, r, re, acc, hn, hf, wg, wu, wd,
           in_sem, w_sem, wd_sem, dsend, drecv, rsend, rrecv):
    me = lax.axis_index("ep")
    barrier = pltpu.get_barrier_semaphore()

    @pl.loop(1, N)
    def _(p):
        pl.semaphore_signal(barrier, 1, device_id={"ep": partner(me, p)}, device_id_type=MESH)

    small = [pltpu.make_async_copy(a, b, in_sem.at[i])
             for i, (a, b) in enumerate(((e_hbm, e_ref), (s_hbm, s_ref), (g_hbm, g_ref), (x_hbm, x_ref)))]
    for c in small:
        c.start()

    def tile(t):
        slot = lax.rem(t, DEPTH)
        cols = pl.ds(pl.multiple_of(t * FT, FT), FT)
        return (pltpu.make_async_copy(wg_hbm.at[:, cols], wg.at[slot], w_sem.at[slot, 0]),
                pltpu.make_async_copy(wu_hbm.at[:, cols], wu.at[slot], w_sem.at[slot, 1]))

    def load(t):
        for c in tile(t):
            c.start()

    for t in range(DEPTH):
        load(t)
    down = pltpu.make_async_copy(wd_hbm, wd, wd_sem)
    down.start()
    for c in small:
        c.wait()

    e, s = e_ref[...], s_ref[...]
    p = jnp.zeros_like(e)
    for b, bit in enumerate(MASK_BITS):
        p += (((e >> bit) & 1) ^ ((me >> bit) & 1)) << b
    key = jnp.where(s < 16, p * 16 + s, -1)
    key4 = jnp.where((s >= 16) & (s < C), p * 4 + s - 16, -1)
    gate = g_ref[...].astype(jnp.bfloat16).astype(jnp.float32)

    row = iota((N * 16, T), 0)
    row4 = (row // 16) * 4 + lax.rem(row, 4)
    quarter = lax.rem(row // 4, 4)
    x = x_ref[...]
    hit = (row == key[0:1]) | (row == key[1:2])
    zs[...] = dot(hit.astype(jnp.bfloat16), x).astype(jnp.bfloat16)
    hit4 = (row4 == key4[0:1]) | (row4 == key4[1:2])
    part = jnp.zeros((N * 16, Q), jnp.float32)
    for q in range(4):
        part += dot((hit4 & (quarter == q)).astype(jnp.bfloat16), x[:, q * Q:(q + 1) * Q])
    zse[...] = part.astype(jnp.bfloat16)
    z[0:16, :] = zs[0:16, :]
    zre[0:16, :] = zse[0:16, :]

    pl.semaphore_wait(barrier, N - 1)

    def remote(src, dst, send, recv, p):
        return pltpu.make_async_remote_copy(
            src, dst, send, recv, device_id={"ep": partner(me, p)}, device_id_type=MESH)

    for g, (first, count, _) in enumerate(GROUPS):
        @pl.loop(max(first, 1), first + count)
        def _(p, g=g):
            b = pl.ds(pl.multiple_of(p * 16, 16), 16)
            remote(zs.at[b], z.at[pl.ds(rows_of(p), 16)], dsend.at[g, 0], drecv.at[g, 0], p).start()
            remote(zse.at[b], zre.at[b], dsend.at[g, 1], drecv.at[g, 1], p).start()

    def whole(g, packed, base, send, recv):
        first, count, rows = GROUPS[g]
        skip = 16 if first == 0 else 0
        start = rows if packed else first * 16
        b = pl.ds(start + skip, count * 16 - skip)
        return remote(base.at[b], base.at[b], send, recv, 1)

    def quarters(shape, along):
        a, b = iota(shape, along), iota(shape, 1 - along)
        same = (a // 16) * 4 + lax.rem(a, 4) == b
        return [(same & (lax.rem(a // 4, 4) == q)).astype(jnp.bfloat16) for q in range(4)]

    def arrive(g):
        first, count, rows = GROUPS[g]
        whole(g, True, z, dsend.at[g, 0], drecv.at[g, 0]).wait_recv()
        whole(g, False, zre, dsend.at[g, 1], drecv.at[g, 1]).wait_recv()
        packed = zre[first * 16:(first + count) * 16, :]
        top = rows + count * 16
        for q, pick in enumerate(quarters((count * 4, count * 16), 1)):
            z[top:top + count * 4, q * Q:(q + 1) * Q] = dot(pick, packed).astype(jnp.bfloat16)

    def gated(g, h, t):
        _, count, rows = GROUPS[g]
        slot = lax.rem(t, DEPTH)
        a = z[rows:rows + count * C, :]
        for n in range(FT // BLOCK):
            cols = slice(n * BLOCK, (n + 1) * BLOCK)
            u = dot(a, wg[slot, :, cols])
            v = dot(a, wu[slot, :, cols])
            h[:, pl.ds(pl.multiple_of(t * FT + n * BLOCK, BLOCK), BLOCK)] = (
                jax.nn.silu(u) * v).astype(jnp.bfloat16)

    def project(g, h):
        first, count, rows = GROUPS[g]

        @pl.loop(0, D // BLOCK)
        def _(n):
            cols = pl.ds(pl.multiple_of(n * BLOCK, BLOCK), BLOCK)
            o[rows:rows + count * C, cols] = dot(h[...], wd[:, cols]).astype(jnp.bfloat16)

        top = rows + count * 16
        part = jnp.zeros((count * 16, Q), jnp.float32)
        for q, pick in enumerate(quarters((count * 16, count * 4), 0)):
            part += dot(pick, o[top:top + count * 4, q * Q:(q + 1) * Q])
        oe[first * 16:(first + count) * 16, :] = part.astype(jnp.bfloat16)

        @pl.loop(max(first, 1), first + count)
        def _(p):
            b = pl.ds(pl.multiple_of(p * 16, 16), 16)
            remote(o.at[pl.ds(rows_of(p), 16)], r.at[b], rsend.at[g, 0], rrecv.at[g, 0], p).start()
            remote(oe.at[b], re.at[b], rsend.at[g, 1], rrecv.at[g, 1], p).start()

    def wait_tile(t):
        for c in tile(t):
            c.wait()

    arrive(0)

    @pl.loop(0, TILES)
    def _(t):
        wait_tile(t)
        gated(0, hn, t)

        @pl.when(t < TILES - DEPTH)
        def _():
            load(t + DEPTH)

    arrive(1)

    @pl.loop(0, TILES)
    def _(i):
        t = TILES - 1 - i

        @pl.when(i >= DEPTH)
        def _():
            wait_tile(t)

        gated(1, hf, t)

        @pl.when(t >= DEPTH)
        def _():
            load(t - DEPTH)

    down.wait()
    project(1, hf)

    arrive(2)

    @pl.loop(0, TILES)
    def _(t):
        @pl.when(t >= DEPTH)
        def _():
            wait_tile(t)

        gated(2, hf, t)

        @pl.when(t < TILES - DEPTH)
        def _():
            load(t + DEPTH)

    project(2, hf)
    project(0, hn)
    r[0:16, :] = o[0:16, :]
    re[0:16, :] = oe[0:16, :]

    for g in (1, 0, 2):
        first, count, _ = GROUPS[g]
        whole(g, False, r, rsend.at[g, 0], rrecv.at[g, 0]).wait_recv()
        whole(g, False, re, rsend.at[g, 1], rrecv.at[g, 1]).wait_recv()
        b = slice(first * 16, (first + count) * 16)
        row = first * 16 + iota((count * 16, T), 0)
        row4 = (row // 16) * 4 + lax.rem(row, 4)
        quarter = lax.rem(row // 4, 4)
        w = jnp.where(row == key[0:1], gate[0:1], 0.0) + jnp.where(row == key[1:2], gate[1:2], 0.0)
        w4 = jnp.where(row4 == key4[0:1], gate[0:1], 0.0) + jnp.where(row4 == key4[1:2], gate[1:2], 0.0)
        w = w.astype(jnp.bfloat16)
        for q in range(4):
            cols = slice(q * Q, (q + 1) * Q)
            mine = jnp.where(quarter == q, w4, 0.0).astype(jnp.bfloat16)
            total = dot(w, r[b, cols], ((0,), (0,))) + dot(mine, re[b, :], ((0,), (0,)))
            if g == 1:
                acc[:, cols] = total
            elif g == 0:
                acc[:, cols] += total
            else:
                y_ref[:, cols] = (acc[:, cols] + total).astype(jnp.bfloat16)

    for g in range(3):
        whole(g, False, zs, dsend.at[g, 0], drecv.at[g, 0]).wait_send()
        whole(g, False, zse, dsend.at[g, 1], drecv.at[g, 1]).wait_send()
        whole(g, True, o, rsend.at[g, 0], rrecv.at[g, 0]).wait_send()
        whole(g, False, oe, rsend.at[g, 1], rrecv.at[g, 1]).wait_send()


def solution(mesh):
    def step(x, expert, slot, gate, w_gate, w_up, w_down):
        bf16 = jnp.bfloat16
        flat = lambda v: v.reshape(T, 2).T
        any_ = pl.BlockSpec(memory_space=pl.ANY)
        vmem = pltpu.VMEM
        y = pl.pallas_call(
            kernel,
            out_shape=jax.ShapeDtypeStruct((T, D), bf16),
            in_specs=[any_] * 7,
            out_specs=pl.BlockSpec(memory_space=pltpu.VMEM),
            scratch_shapes=[
                vmem((T, D), bf16),
                vmem((2, T), jnp.int32),
                vmem((2, T), jnp.int32),
                vmem((2, T), jnp.float32),
                vmem((N * 16, D), bf16),
                vmem((N * 16, Q), bf16),
                vmem((N * C, D), bf16),
                vmem((N * 16, Q), bf16),
                vmem((N * C, D), bf16),
                vmem((N * 16, Q), bf16),
                vmem((N * 16, D), bf16),
                vmem((N * 16, Q), bf16),
                vmem((T, D), jnp.float32),
                vmem((16 * C, FF), bf16),
                vmem((8 * C, FF), bf16),
                vmem((DEPTH, D, FT), bf16),
                vmem((DEPTH, D, FT), bf16),
                vmem((FF, D), bf16),
                pltpu.SemaphoreType.DMA((4,)),
                pltpu.SemaphoreType.DMA((DEPTH, 2)),
                pltpu.SemaphoreType.DMA,
                pltpu.SemaphoreType.DMA((3, 2)),
                pltpu.SemaphoreType.DMA((3, 2)),
                pltpu.SemaphoreType.DMA((3, 2)),
                pltpu.SemaphoreType.DMA((3, 2)),
            ],
            compiler_params=pltpu.CompilerParams(
                collective_id=0, has_side_effects=True, vmem_limit_bytes=67043328
            ),
            name="moe",
        )(x.reshape(T, D), flat(expert), flat(slot), flat(gate), w_gate[0], w_up[0], w_down[0])
        return y.reshape(1, 1, T, D)

    row = P("dp", "ep", None, None)
    weight = P("ep", None, None)
    return jax.shard_map(
        step, mesh=mesh, in_specs=(row,) * 4 + (weight,) * 3, out_specs=row, check_vma=False
    )
```

time: 218 us -> 131 us (0.60)
  Pallas kernels: 0 us -> 128 us
  matrix products: 92.9 us -> 0 us
  blocking collectives: 64.2 us -> 0 us
  waiting for transfers between devices: 49 us -> 0 us
  local copies, waits for them, and re-layouts: 8.85 us -> 2.06 us
  starting transfers between devices: 2.77 us -> 0 us
    pallas_call x0 -> x1, Pallas kernels: none -> 128 us  [step(): pl.pallas_call(kernel, out_shape=jax.ShapeDtypeStruct((T, D), bf16), in_s...]
    dot_general x7 -> x0, matrix products: 92.9 us -> none  [einsum(): return jnp.einsum(form, a.astype(jnp.float32), b.astype(jnp.float32))]
    another operation x1 -> x0, blocking collectives: 64.2 us -> none  [placed(): return lax.with_sharding_constraint(v, NamedSharding(mesh, P(*spec)))]
    another operation x1 -> x0, waiting for transfers between devices: 49 us -> none  [placed(): return lax.with_sharding_constraint(v, NamedSharding(mesh, P(*spec)))]
    another operation x2 -> x0, local copies, waits for them, and re-layouts: 3.6 us -> none  [placed(): return lax.with_sharding_constraint(v, NamedSharding(mesh, P(*spec)))]
    another operation x1 -> x0, starting transfers between devices: 2.77 us -> none  [placed(): return lax.with_sharding_constraint(v, NamedSharding(mesh, P(*spec)))]
    dot_general x2 -> x0, local copies, waits for them, and re-layouts: 2.71 us -> none  [einsum(): return jnp.einsum(form, a.astype(jnp.float32), b.astype(jnp.float32))]
  transfers between devices with their start and end apart: 1 -> 0, of which waited for: 1 -> 0; matrix products, arithmetic and copies ran while one was open for 3% -> 0% of each run, Pallas kernels for 0% -> 0%
where the time goes in v1:
time: 131 us; the launch traced here: 130 us
  Pallas kernels  128 us (98%)
  local copies, waits for them, and re-layouts  2.06 us (2%)
    pallas_call x1, Pallas kernels, step(): pl.pallas_call(kernel, out_shape=jax.ShapeDtypeStruct((T, D), bf16), in_s...  128 us

profile of v1, /device:TPU:0, one launch (start us, length us, event | category | flops | bytes accessed | tf_op | source)
XLA Modules:
  0.0 130.4 jit_solution(8931057946554512967)
XLA Ops:
  0.0 128.3 %moe.1 = bf16[256,1536]{1,0:T(8,128)(2,1)} custom-call(bf16[256,1536]{1,0:T(8,128)(2,1)} %bitcast.18, s32[2,256]{1,0:T(2,128)} %bitcast.19, s32[2,256]{1,0:T(2,128)} %bitcast.20, f32[2,256]{1,0:T(2,128)} %bitcast.21, bf16[1536,9216]{1,0:T(8,128)(2,1)} %bitcast.14, bf16[1536,9216]{1,0:T(8,128)(2,1)} %bitcast.15, bf16[9216,1536]{1,0:T(8,128)(2,1)} %bitcast.16), custom_call_target="tpu_custom_call" | custom-call | tf_op jit(solution)/shard_map/moe/pallas_call | solution.py:253
  128.3 2.1 %copy.9 = bf16[1,1,256,1536]{3,2,1,0:T(8,128)(2,1)} copy(bf16[1,1,256,1536]{3,2,1,0:T(8,128)(2,1)} %bitcast.17) | data formatting | bytes 1572864
